TPU v7x, 32 devices: a whole 2x2x4 slice. The times are simulated.
32 devices in a mesh: groups: 2 (over y), blk: 4 (over z), desc: 2 (over x), half: 2 (over core).
Axes of the slice: x: 2, y: 2, z: 4, core: 2. Of those that a mesh axis runs over, the one named last changes fastest.
Arguments:
- descriptors: bfloat16 [8, 2048, 128], P(('groups', 'blk'), ('desc', 'half')), parts along dimension 0, may hold values from -0.5 to 0.5
Outputs:
- best_dist: float32 [3, 8, 2048], P(None, ('groups', 'blk'), 'desc'), parts along dimension 1
- second_dist: float32 [3, 8, 2048], P(None, ('groups', 'blk'), 'desc'), parts along dimension 1
There are 2 independent parts, one for each index of `groups`. A program takes and returns all parts, laid end to end along the dimension named above; each array names one. Nothing has to cross between parts.
All inputs are finite; a program needn't handle non-finite values.
Results may differ from a plain program's by a relative error of at most 0.0003.
Values may be sent and summed in bfloat16 or wider, within the bound.
A program may use at most 64 MiB of HBM per device.

v0:
```python
import functools

import jax
import jax.numpy as jnp
from jax import lax
from jax.experimental import pallas as pl
from jax.experimental.pallas import tpu as pltpu
from jax.sharding import PartitionSpec as P

MESH = pl.DeviceIdType.MESH


def combine(lo_a, se_a, lo_b, se_b):
    return (
        jnp.minimum(lo_a, lo_b),
        jnp.minimum(jnp.maximum(lo_a, lo_b), jnp.minimum(se_a, se_b)),
    )


def nt_dot(a, b):
    return lax.dot_general(a, b, (((1,), (1,)), ((), ())), preferred_element_type=jnp.float32)


def kernel(
    n, D, H, CH, x_hbm, best_ref, second_ref, norm_ref,
    x_ref, buf, q, qn, low, sec, mine, inbox,
    x_sem, f_send, z_send, z_recv, q_send, q_recv, p_send, p_recv,
):
    R = x_hbm.shape[0]
    load = pltpu.make_async_copy(x_hbm, x_ref, x_sem)
    load.start()
    CR = R // CH
    share = H * R
    Q = D * share
    TQ = min(256, share)
    i = lax.axis_index("blk")
    d = lax.axis_index("desc")
    h = lax.axis_index("half")
    others = [(dd, hh) for dd in range(D) for hh in range(H) if (dd, hh) != (0, 0)]

    def peer(dd, hh):
        return {"desc": lax.rem(d + dd, D), "half": lax.rem(h + hh, H)}

    def rows_of(d_at, h_at):
        return pl.ds(pl.multiple_of((d_at * H + h_at) * R, R), R)

    def chunk(c):
        return pl.ds(pl.multiple_of(c * CR, CR), CR)

    def inside(j):
        return (j >= 0) & (j < n)

    barrier = pltpu.get_barrier_semaphore()
    for step in (1, -1):
        @pl.when(inside(i + step))
        def _():
            pl.semaphore_signal(barrier, inc=1, device_id={"blk": i + step}, device_id_type=MESH)
    for dd, hh in others:
        pl.semaphore_signal(barrier, inc=1, device_id=peer(dd, hh), device_id_type=MESH)
    at_end = ((i == 0) | (i == n - 1)) & (n > 2)
    opposite = n - 1 - i

    @pl.when(at_end)
    def _():
        pl.semaphore_signal(barrier, inc=1, device_id={"blk": opposite}, device_id_type=MESH)

    links = jnp.where(at_end, 1, 0) + jnp.where(inside(i + 1), 1, 0) + jnp.where(inside(i - 1), 1, 0)
    low[...] = jnp.full(low.shape, jnp.inf, jnp.float32)
    sec[...] = jnp.full(sec.shape, jnp.inf, jnp.float32)
    load.wait()
    pl.semaphore_wait(barrier, len(others) + links)

    def own_copy(way, c):
        step = 1 - 2 * way
        return pltpu.make_async_remote_copy(
            src_ref=x_ref.at[chunk(c)], dst_ref=buf.at[i, chunk(c)],
            send_sem=z_send.at[way, i, c], recv_sem=z_recv.at[i, c],
            device_id={"blk": i + step}, device_id_type=MESH,
        )

    def relay_copy(way, j, c):
        step = 1 - 2 * way
        return pltpu.make_async_remote_copy(
            src_ref=buf.at[j, chunk(c)], dst_ref=buf.at[j, chunk(c)],
            send_sem=z_send.at[way, j, c], recv_sem=z_recv.at[j, c],
            device_id={"blk": i + step}, device_id_type=MESH,
        )

    def far_copy(c):
        return pltpu.make_async_remote_copy(
            src_ref=x_ref.at[chunk(c)], dst_ref=buf.at[i, chunk(c)],
            send_sem=f_send.at[c], recv_sem=z_recv.at[i, c],
            device_id={"blk": opposite}, device_id_type=MESH,
        )

    for c in range(CH):
        for way in (0, 1):
            @pl.when(inside(i + 1 - 2 * way))
            def _():
                own_copy(way, c).start()

    @pl.when(at_end)
    def _():
        for c in range(CH):
            far_copy(c).start()

    mine_rows = rows_of(d, h)

    def query_copy(dd, hh):
        return pltpu.make_async_remote_copy(
            src_ref=x_ref, dst_ref=q.at[mine_rows],
            send_sem=q_send.at[dd * H + hh], recv_sem=q_recv.at[dd * H + hh],
            device_id=peer(dd, hh), device_id_type=MESH,
        )

    def query_relay(dd, hh):
        src_rows = rows_of(lax.rem(d + D - dd, D), h)
        return pltpu.make_async_remote_copy(
            src_ref=q.at[src_rows], dst_ref=q.at[src_rows],
            send_sem=q_send.at[dd * H + hh], recv_sem=q_recv.at[dd * H + hh],
            device_id=peer(0, hh), device_id_type=MESH,
        )

    for dd in range(1, D):
        query_copy(dd, 0).start()
    for hh in range(1, H):
        query_copy(0, hh).start()

    q[mine_rows, :] = x_ref[...]

    def each(steps, body):
        def over_steps(s, carry):
            def over_chunks(c, carry):
                def over_ways(way, carry):
                    body(s, c, way, i - s + 2 * s * way)
                    return carry

                return lax.fori_loop(0, 2, over_ways, carry)

            return lax.fori_loop(0, CH, over_chunks, carry)

        lax.fori_loop(1, 1 + steps, over_steps, 0)

    def passes(way, s, j):
        return inside(j) & inside(i + 1 - 2 * way) & (s + 1 < n - 1)

    def relay(s, c, way, j):
        @pl.when(passes(way, s, j) & (s < n))
        def _():
            copy = relay_copy(way, j, c)
            copy.wait_recv()
            copy.start()

    each(1, relay)

    for dd in range(1, D):
        query_copy(dd, 0).wait_recv()
        for hh in range(1, H):
            query_relay(dd, hh).start()
    for dd in range(D):
        for hh in range(1, H):
            query_copy(dd, hh).wait_recv()

    ones = jnp.ones((8, q.shape[1]), jnp.bfloat16)
    for t in range(D):
        wide = q[t * share : (t + 1) * share, :].astype(jnp.float32)
        square = wide * wide
        head = square.astype(jnp.bfloat16)
        tail = (square - head.astype(jnp.float32)).astype(jnp.bfloat16)
        qn[t] = nt_dot(ones, head) + nt_dot(ones, tail)

    def result_copy(k, dd, hh):
        return pltpu.make_async_remote_copy(
            src_ref=mine.at[k, lax.rem(d + dd, D)], dst_ref=inbox.at[k, dd * H + hh],
            send_sem=p_send.at[k, dd * H + hh], recv_sem=p_recv.at[k, dd * H + hh],
            device_id=peer(dd, hh), device_id_type=MESH,
        )

    def work(s, c, way, j):
        relay(s + 1, c, way, j - 1 + 2 * way)

        @pl.when(inside(j))
        def _():
            @pl.when(jnp.logical_not(passes(way, s, j)))
            def _():
                relay_copy(way, j, c).wait_recv()

            k = jnp.where(way == 0, s, n - s) - 1
            piece = buf[j, chunk(c), :]
            wide = piece.astype(jnp.float32)
            norms = jnp.sum(wide * wide, axis=1, keepdims=True)
            scaled = (wide * -2.0).astype(jnp.bfloat16)
            for t in range(Q // TQ):
                lanes = slice(t * TQ, (t + 1) * TQ)
                part = nt_dot(scaled, q[lanes, :]) + norms
                lo, se = low[k, :, lanes], sec[k, :, lanes]
                for r in range(CR // 8):
                    value = part[8 * r : 8 * r + 8]
                    se = jnp.minimum(se, jnp.maximum(lo, value))
                    lo = jnp.minimum(lo, value)
                low[k, :, lanes] = lo
                sec[k, :, lanes] = se

            @pl.when(c == CH - 1)
            def _():
                for t in range(D):
                    lanes = slice(t * share, (t + 1) * share)
                    lo, se = low[k, :, lanes], sec[k, :, lanes]
                    for turn in (4, 2, 1):
                        lo, se = combine(
                            lo, se, pltpu.roll(lo, turn, 0), pltpu.roll(se, turn, 0)
                        )
                    mine[k, t, 0:1, :] = lo[0:1]
                    mine[k, t, 1:2, :] = se[0:1]
                for dd, hh in reversed(others):
                    result_copy(k, dd, hh).start()

    each(n - 1, work)

    def finish(k, carry):
        lo, se = mine[k, d, 0:1, :], mine[k, d, 1:2, :]
        for dd, hh in others:
            result_copy(k, dd, hh).wait_recv()
            at = dd * H + hh
            lo, se = combine(lo, se, inbox[k, at, 0:1, :], inbox[k, at, 1:2, :])
        norms = qn[d, 0:1, :]
        best_ref[k] = lo
        second_ref[k] = se
        norm_ref[...] = norms
        return carry

    def sent_relay(s, c, way, j):
        @pl.when(passes(way, s, j))
        def _():
            relay_copy(way, j, c).wait_send()

    each(n - 1, sent_relay)
    for c in range(CH):
        for way in (0, 1):
            @pl.when(inside(i + 1 - 2 * way))
            def _():
                own_copy(way, c).wait_send()

    @pl.when(at_end)
    def _():
        for c in range(CH):
            far_copy(c).wait_send()

    for dd in range(1, D):
        query_copy(dd, 0).wait_send()
        for hh in range(1, H):
            query_relay(dd, hh).wait_send()
    for hh in range(1, H):
        query_copy(0, hh).wait_send()

    lax.fori_loop(0, n - 1, finish, 0)

    def sent_results(k, carry):
        for dd, hh in others:
            result_copy(k, dd, hh).wait_send()
        return carry

    lax.fori_loop(0, n - 1, sent_results, 0)


def solution(mesh):
    n, D, H = mesh.shape["blk"], mesh.shape["desc"], mesh.shape["half"]

    def per_device(descriptors):
        block = descriptors[0]
        R, depth = block.shape
        CH = 2 if R % 32 == 0 else 1
        share = H * R
        out = pltpu.VMEM((n - 1, 1, share), jnp.float32)
        vmem = pl.BlockSpec(memory_space=pltpu.VMEM)
        lo, se, norms = pl.pallas_call(
            functools.partial(kernel, n, D, H, CH),
            out_shape=(out, out, pltpu.VMEM((1, share), jnp.float32)),
            in_specs=[pl.BlockSpec(memory_space=pltpu.HBM)],
            out_specs=(vmem, vmem, vmem),
            scratch_shapes=[
                pltpu.VMEM((R, depth), jnp.bfloat16),
                pltpu.VMEM((n, R, depth), jnp.bfloat16),
                pltpu.VMEM((D * share, depth), jnp.bfloat16),
                pltpu.VMEM((D, 8, share), jnp.float32),
                pltpu.VMEM((n - 1, 8, D * share), jnp.float32),
                pltpu.VMEM((n - 1, 8, D * share), jnp.float32),
                pltpu.VMEM((n - 1, D, 2, share), jnp.float32),
                pltpu.VMEM((n - 1, D * H, 2, share), jnp.float32),
                pltpu.SemaphoreType.DMA,
                pltpu.SemaphoreType.DMA((CH,)),
                pltpu.SemaphoreType.DMA((2, n, CH)),
                pltpu.SemaphoreType.DMA((n, CH)),
                pltpu.SemaphoreType.DMA((D * H,)),
                pltpu.SemaphoreType.DMA((D * H,)),
                pltpu.SemaphoreType.DMA((n - 1, D * H)),
                pltpu.SemaphoreType.DMA((n - 1, D * H)),
            ],
            compiler_params=pltpu.CompilerParams(collective_id=0, has_side_effects=True),
        )(block)
        return norms + lo, norms + se

    in_specs = (P(("groups", "blk"), ("desc", "half"), None),)
    out_specs = (P(None, ("groups", "blk"), "desc"), P(None, ("groups", "blk"), "desc"))
    return jax.shard_map(
        per_device, mesh=mesh, in_specs=in_specs, out_specs=out_specs, check_vma=False
    )
```

profile of v0, /device:TPU:0, one launch (start us, length us, event | category | flops | bytes accessed | tf_op | source)
XLA Modules:
  0.0 21.2 jit_solution(10977022503638096271)
XLA Ops:
  0.6 19.9 %shard_map.30 = (f32[3,1,1024]{2,1,0:T(1,128)S(1)}, f32[3,1,1024]{2,1,0:T(1,128)S(1)}, f32[1,1024]{1,0:T(1,128)S(1)}) custom-call(bf16[512,128]{1,0:T(8,128)(2,1)} %bitcast.3), custom_call_target="tpu_custom_call" | custom-call | tf_op jit(solution)/shard_map/pallas_call | solution.py:276
  20.6 0.6 %broadcast_add_fusion = (f32[3,1,1024]{2,1,0:T(1,128)}, f32[3,1,1024]{2,1,0:T(1,128)}) fusion(f32[3,1,1024]{2,1,0:T(1,128)S(1)} %get-tuple-element.7, f32[1024]{0:T(1024)S(1)} %bitcast.2, f32[3,1,1024]{2,1,0:T(1,128)S(1)} %get-tuple-element.6), kind=kLoop, calls=%fused_computation | loop fusion | flops 6144 | bytes 53248 | tf_op jit(solution)/shard_map/add | solution.py:301
where the time goes:
time: 21.4 us; the launch traced here: 21.2 us
  Pallas kernels  19.9 us (93%)
  between operations  0.64 us (3%)
  other arithmetic  0.63 us (3%)
    pallas_call x1, Pallas kernels, per_device(): pl.pallas_call(functools.partial(kernel, n, D, H, CH), out_shape=(out, ou...  19.9 us
    add x1, other arithmetic, per_device(): return (norms + lo, norms + se)  0.63 us

commit v1 on v0

v1 whole, which is shorter than its diff:
```python
import functools

import jax
import jax.numpy as jnp
from jax import lax
from jax.experimental import pallas as pl
from jax.experimental.pallas import tpu as pltpu
from jax.sharding import PartitionSpec as P

MESH = pl.DeviceIdType.MESH


def combine(lo_a, se_a, lo_b, se_b):
    return (
        jnp.minimum(lo_a, lo_b),
        jnp.minimum(jnp.maximum(lo_a, lo_b), jnp.minimum(se_a, se_b)),
    )


def nt_dot(a, b):
    return lax.dot_general(a, b, (((1,), (1,)), ((), ())), preferred_element_type=jnp.float32)


def fold(part, lo, se):
    for r in range(part.shape[0] // 8):
        value = part[8 * r : 8 * r + 8]
        se = jnp.minimum(se, jnp.maximum(lo, value))
        lo = jnp.minimum(lo, value)
    return lo, se


def across_rows(lo, se):
    for turn in (4, 2, 1):
        lo, se = combine(lo, se, pltpu.roll(lo, turn, 0), pltpu.roll(se, turn, 0))
    return lo[0:1], se[0:1]


def kernel(
    n, D, H, CH, x_hbm, best_ref, second_ref, norm_ref,
    x_ref, buf, q, sn, low, sec, mine, inbox, turned, returned,
    x_sem, go, z_send, z_recv, q_send, q_recv, p_send, p_recv, m_send, m_recv,
):
    R = x_hbm.shape[0]
    load = pltpu.make_async_copy(x_hbm, x_ref, x_sem)
    load.start()
    CR = R // CH
    share = H * R
    Q = D * share
    TQ = min(256, share)
    T = n // 2
    i = lax.axis_index("blk")
    d = lax.axis_index("desc")
    h = lax.axis_index("half")
    others = [(dd, hh) for dd in range(D) for hh in range(H) if (dd, hh) != (0, 0)]

    if n % 2 == 0:
        hosts_tie = (i < T) == (lax.rem(lax.rem(i, T), 2) == 0)
    else:
        hosts_tie = i >= 0

    def hosting(s):
        return (2 * s != n) | hosts_tie

    def visiting(s):
        if n % 2 == 0:
            return (2 * s != n) | jnp.logical_not(hosts_tie)
        return 2 * s != n

    def guest_of(s):
        return lax.rem(i - s + n, n)

    def host_of(s):
        return lax.rem(i + s, n)

    def peer(dd, hh):
        return {"desc": lax.rem(d + dd, D), "half": lax.rem(h + hh, H)}

    def rows_of(d_at, h_at):
        return pl.ds(pl.multiple_of((d_at * H + h_at) * R, R), R)

    def chunk(c):
        return pl.ds(pl.multiple_of(c * CR, CR), CR)

    barrier = pltpu.get_barrier_semaphore()

    def greet(s, met):
        for active, at in ((visiting(s), host_of(s)), (hosting(s), guest_of(s))):
            @pl.when(active & (i < at))
            def _():
                pl.semaphore_signal(barrier, inc=1, device_id={"blk": at}, device_id_type=MESH)

            met = met + jnp.where(active & (at < i), 1, 0)
        return met

    met = lax.fori_loop(1, T + 1, greet, jnp.int32(0))
    for dd, hh in others:
        pl.semaphore_signal(barrier, inc=1, device_id=peer(dd, hh), device_id_type=MESH)
    pl.semaphore_wait(barrier, len(others) + met)

    def invite(s, carry):
        at = guest_of(s)

        @pl.when(hosting(s) & (at < i))
        def _():
            pl.semaphore_signal(go.at[s - 1], inc=1, device_id={"blk": at}, device_id_type=MESH)

        return carry

    lax.fori_loop(1, T + 1, invite, 0)

    def move(s, c):
        return pltpu.make_async_remote_copy(
            src_ref=x_ref.at[chunk(c)], dst_ref=buf.at[s - 1, chunk(c)],
            send_sem=z_send.at[s - 1, c], recv_sem=z_recv.at[s - 1, c],
            device_id={"blk": host_of(s)}, device_id_type=MESH,
        )

    mine_rows = rows_of(d, h)

    def query_copy(dd, hh):
        return pltpu.make_async_remote_copy(
            src_ref=x_ref, dst_ref=q.at[mine_rows],
            send_sem=q_send.at[dd * H + hh], recv_sem=q_recv.at[dd * H + hh],
            device_id=peer(dd, hh), device_id_type=MESH,
        )

    def query_relay(dd, hh):
        src_rows = rows_of(lax.rem(d + D - dd, D), h)
        return pltpu.make_async_remote_copy(
            src_ref=q.at[src_rows], dst_ref=q.at[src_rows],
            send_sem=q_send.at[dd * H + hh], recv_sem=q_recv.at[dd * H + hh],
            device_id=peer(0, hh), device_id_type=MESH,
        )

    load.wait()

    def move_down(s, carry):
        @pl.when(visiting(s) & (host_of(s) < i))
        def _():
            for c in range(CH):
                move(s, c).start()

        return carry

    lax.fori_loop(1, T + 1, move_down, 0)
    for dd in range(1, D):
        query_copy(dd, 0).start()
    for hh in range(1, H):
        query_copy(0, hh).start()
    q[mine_rows, :] = x_ref[...]

    def move_up(s, carry):
        @pl.when(visiting(s) & (host_of(s) > i))
        def _():
            pl.semaphore_wait(go.at[s - 1], 1)
            for c in range(CH):
                move(s, c).start()

        return carry

    lax.fori_loop(1, T + 1, move_up, 0)

    for dd in range(1, D):
        query_copy(dd, 0).wait_recv()
        for hh in range(1, H):
            query_relay(dd, hh).start()
    for dd in range(D):
        for hh in range(1, H):
            query_copy(dd, hh).wait_recv()

    def widen(t, carry):
        rows = pl.ds(pl.multiple_of(t * TQ, TQ), TQ)
        wide = q[rows, :].astype(jnp.float32)
        sn[rows, :] = jnp.broadcast_to(jnp.sum(wide * wide, axis=1, keepdims=True), (TQ, 128))
        return carry

    lax.fori_loop(0, Q // TQ, widen, 0)

    def result_copy(s, dd, hh):
        return pltpu.make_async_remote_copy(
            src_ref=mine.at[s - 1, lax.rem(d + dd, D)], dst_ref=inbox.at[s - 1, dd * H + hh],
            send_sem=p_send.at[s - 1, dd * H + hh], recv_sem=p_recv.at[s - 1, dd * H + hh],
            device_id=peer(dd, hh), device_id_type=MESH,
        )

    def return_copy(s, hh):
        return pltpu.make_async_remote_copy(
            src_ref=turned.at[s - 1], dst_ref=returned.at[s - 1, hh],
            send_sem=m_send.at[s - 1, hh], recv_sem=m_recv.at[s - 1, hh],
            device_id={"blk": guest_of(s), "half": lax.rem(h + hh, H)}, device_id_type=MESH,
        )

    def step_of(u):
        return jnp.where(2 * i < n, T - u, u + 1)

    inf = functools.partial(jnp.full, fill_value=jnp.inf, dtype=jnp.float32)

    def work(u, carry):
        s = step_of(u)

        @pl.when(hosting(s))
        def _():
            low[...] = inf(low.shape)
            sec[...] = inf(sec.shape)

            def part_of(c, carry):
                move(s, c).wait_recv()
                wide = buf[s - 1, chunk(c), :].astype(jnp.float32)
                norms = jnp.sum(wide * wide, axis=1, keepdims=True)
                scaled = (wide * -2.0).astype(jnp.bfloat16)
                for t in range(Q // TQ):
                    lanes = slice(t * TQ, (t + 1) * TQ)
                    lo, se = fold(nt_dot(scaled, q[lanes, :]) + norms, low[:, lanes], sec[:, lanes])
                    low[:, lanes] = lo
                    sec[:, lanes] = se
                lo, se = inf((8, CR)), inf((8, CR))
                for t in range(Q // TQ):
                    rows = slice(t * TQ, (t + 1) * TQ)
                    lo, se = fold(nt_dot(q[rows, :], scaled) + sn[rows, 0:1], lo, se)
                lo, se = across_rows(lo, se)
                turned[s - 1, c, 0:1, :] = lo
                turned[s - 1, c, 1:2, :] = se
                return carry

            lax.fori_loop(0, CH, part_of, 0)
            for t in range(D):
                lanes = slice(t * share, (t + 1) * share)
                lo, se = across_rows(low[:, lanes], sec[:, lanes])
                mine[s - 1, t, 0:1, :] = lo
                mine[s - 1, t, 1:2, :] = se
            for dd, hh in reversed(others):
                result_copy(s, dd, hh).start()
            for hh in range(H):
                return_copy(s, hh).start()

        return carry

    lax.fori_loop(0, T, work, 0)

    own = q[pl.ds(pl.multiple_of(d * share, share), share), :].astype(jnp.float32)
    square = own * own
    head = square.astype(jnp.bfloat16)
    tail = (square - head.astype(jnp.float32)).astype(jnp.bfloat16)
    ones = jnp.ones((8, q.shape[1]), jnp.bfloat16)
    norm_ref[...] = (nt_dot(ones, head) + nt_dot(ones, tail))[0:1]

    def sent(s, carry):
        @pl.when(visiting(s))
        def _():
            for c in range(CH):
                move(s, c).wait_send()

        return carry

    lax.fori_loop(1, T + 1, sent, 0)
    for dd in range(1, D):
        query_copy(dd, 0).wait_send()
        for hh in range(1, H):
            query_relay(dd, hh).wait_send()
    for hh in range(1, H):
        query_copy(0, hh).wait_send()

    def finish(u, carry):
        s = step_of(u)

        @pl.when(visiting(s))
        def _():
            for hh in range(H):
                return_copy(s, hh).wait_recv()
            for hh in range(H):
                for c in range(CH):
                    at = lax.rem(h + H - hh, H) * CH + c
                    lanes = pl.ds(pl.multiple_of(at * CR, CR), CR)
                    best_ref[n - s - 1, :, lanes] = returned[s - 1, hh, c, 0:1, :]
                    second_ref[n - s - 1, :, lanes] = returned[s - 1, hh, c, 1:2, :]

        @pl.when(hosting(s))
        def _():
            lo, se = mine[s - 1, d, 0:1, :], mine[s - 1, d, 1:2, :]
            for dd, hh in others:
                result_copy(s, dd, hh).wait_recv()
                at = dd * H + hh
                lo, se = combine(lo, se, inbox[s - 1, at, 0:1, :], inbox[s - 1, at, 1:2, :])
            best_ref[s - 1] = lo
            second_ref[s - 1] = se

        return carry

    lax.fori_loop(0, T, finish, 0)

    def sent_results(s, carry):
        @pl.when(hosting(s))
        def _():
            for dd, hh in others:
                result_copy(s, dd, hh).wait_send()
            for hh in range(H):
                return_copy(s, hh).wait_send()

        return carry

    lax.fori_loop(1, T + 1, sent_results, 0)


def solution(mesh):
    n, D, H = mesh.shape["blk"], mesh.shape["desc"], mesh.shape["half"]
    T = n // 2

    def per_device(descriptors):
        block = descriptors[0]
        R, depth = block.shape
        CH = 2 if R % 32 == 0 else 1
        CR = R // CH
        share = H * R
        out = pltpu.VMEM((n - 1, 1, share), jnp.float32)
        vmem = pl.BlockSpec(memory_space=pltpu.VMEM)
        lo, se, norms = pl.pallas_call(
            functools.partial(kernel, n, D, H, CH),
            out_shape=(out, out, pltpu.VMEM((1, share), jnp.float32)),
            in_specs=[pl.BlockSpec(memory_space=pltpu.HBM)],
            out_specs=(vmem, vmem, vmem),
            scratch_shapes=[
                pltpu.VMEM((R, depth), jnp.bfloat16),
                pltpu.VMEM((T, R, depth), jnp.bfloat16),
                pltpu.VMEM((D * share, depth), jnp.bfloat16),
                pltpu.VMEM((D * share, 128), jnp.float32),
                pltpu.VMEM((8, D * share), jnp.float32),
                pltpu.VMEM((8, D * share), jnp.float32),
                pltpu.VMEM((T, D, 2, share), jnp.float32),
                pltpu.VMEM((T, D * H, 2, share), jnp.float32),
                pltpu.VMEM((T, CH, 2, CR), jnp.float32),
                pltpu.VMEM((T, H, CH, 2, CR), jnp.float32),
                pltpu.SemaphoreType.DMA,
                pltpu.SemaphoreType.REGULAR((T,)),
                pltpu.SemaphoreType.DMA((T, CH)),
                pltpu.SemaphoreType.DMA((T, CH)),
                pltpu.SemaphoreType.DMA((D * H,)),
                pltpu.SemaphoreType.DMA((D * H,)),
                pltpu.SemaphoreType.DMA((T, D * H)),
                pltpu.SemaphoreType.DMA((T, D * H)),
                pltpu.SemaphoreType.DMA((T, H)),
                pltpu.SemaphoreType.DMA((T, H)),
            ],
            compiler_params=pltpu.CompilerParams(collective_id=0, has_side_effects=True),
        )(block)
        return norms + lo, norms + se

    in_specs = (P(("groups", "blk"), ("desc", "half"), None),)
    out_specs = (P(None, ("groups", "blk"), "desc"), P(None, ("groups", "blk"), "desc"))
    return jax.shard_map(
        per_device, mesh=mesh, in_specs=in_specs, out_specs=out_specs, check_vma=False
    )
```

time: 21.4 us -> 19.1 us (0.89)
  Pallas kernels: 19.9 us -> 17.6 us
    pallas_call x1, Pallas kernels: 19.9 us -> 17.6 us  [per_device(): pl.pallas_call(functools.partial(kernel, n, D, H, CH), out_shape=(out, ou...]
where the time goes in v1:
time: 19.1 us; the launch traced here: 18.9 us
  Pallas kernels  17.6 us (92%)
  between operations  0.64 us (3%)
  other arithmetic  0.63 us (3%)
    pallas_call x1, Pallas kernels, per_device(): pl.pallas_call(functools.partial(kernel, n, D, H, CH), out_shape=(out, ou...  17.6 us
    add x1, other arithmetic, per_device(): return (norms + lo, norms + se)  0.63 us

profile of v1, /device:TPU:0, one launch (start us, length us, event | category | flops | bytes accessed | tf_op | source)
XLA Modules:
  0.0 18.9 jit_solution(15840485816946626873)
XLA Ops:
  0.6 17.6 %shard_map.30 = (f32[3,1,1024]{2,1,0:T(1,128)S(1)}, f32[3,1,1024]{2,1,0:T(1,128)S(1)}, f32[1,1024]{1,0:T(1,128)S(1)}) custom-call(bf16[512,128]{1,0:T(8,128)(2,1)} %bitcast.3), custom_call_target="tpu_custom_call" | custom-call | tf_op jit(solution)/shard_map/pallas_call | solution.py:316
  18.3 0.6 %broadcast_add_fusion = (f32[3,1,1024]{2,1,0:T(1,128)}, f32[3,1,1024]{2,1,0:T(1,128)}) fusion(f32[3,1,1024]{2,1,0:T(1,128)S(1)} %get-tuple-element.7, f32[1024]{0:T(1024)S(1)} %bitcast.2, f32[3,1,1024]{2,1,0:T(1,128)S(1)} %get-tuple-element.6), kind=kLoop, calls=%fused_computation | loop fusion | flops 6144 | bytes 53248 | tf_op jit(solution)/shard_map/add | solution.py:345

commit v2 on v1

--- a/solution.py
+++ b/solution.py
@@ -21,12 +21,20 @@
     return lax.dot_general(a, b, (((1,), (1,)), ((), ())), preferred_element_type=jnp.float32)
 
 
-def fold(part, lo, se):
+def fold(part, norms, lo, se):
+    wide = part.shape[1] // norms.shape[1]
+    kept = [(lo, se), None]
     for r in range(part.shape[0] // 8):
-        value = part[8 * r : 8 * r + 8]
-        se = jnp.minimum(se, jnp.maximum(lo, value))
-        lo = jnp.minimum(lo, value)
-    return lo, se
+        rows = slice(8 * r, 8 * r + 8)
+        value = part[rows] + jnp.concatenate([norms[rows]] * wide, axis=1)
+        if kept[r % 2] is None:
+            kept[r % 2] = (value, jnp.full_like(value, jnp.inf))
+        else:
+            lo, se = kept[r % 2]
+            kept[r % 2] = (jnp.minimum(lo, value), jnp.minimum(se, jnp.maximum(lo, value)))
+    if kept[1] is None:
+        return kept[0]
+    return combine(*kept[0], *kept[1])
 
 
 def across_rows(lo, se):
@@ -37,8 +45,8 @@
 
 def kernel(
     n, D, H, CH, x_hbm, best_ref, second_ref, norm_ref,
-    x_ref, buf, q, sn, low, sec, mine, inbox, turned, returned,
-    x_sem, go, z_send, z_recv, q_send, q_recv, p_send, p_recv, m_send, m_recv,
+    x_ref, buf, q, q2, sn, low, sec, mine, inbox, turned, returned,
+    x_sem, go, go_q, z_send, z_recv, q_send, q_recv, p_send, p_recv, m_send, m_recv,
 ):
     R = x_hbm.shape[0]
     load = pltpu.make_async_copy(x_hbm, x_ref, x_sem)
@@ -93,9 +101,13 @@
         return met
 
     met = lax.fori_loop(1, T + 1, greet, jnp.int32(0))
-    for dd, hh in others:
-        pl.semaphore_signal(barrier, inc=1, device_id=peer(dd, hh), device_id_type=MESH)
-    pl.semaphore_wait(barrier, len(others) + met)
+    for dd in range(1, D):
+        @pl.when(d + dd < D)
+        def _():
+            pl.semaphore_signal(barrier, inc=1, device_id={"desc": d + dd}, device_id_type=MESH)
+    for hh in range(1, H):
+        pl.semaphore_signal(barrier, inc=1, device_id=peer(0, hh), device_id_type=MESH)
+    pl.semaphore_wait(barrier, H - 1 + d + met)
 
     def invite(s, carry):
         at = guest_of(s)
@@ -107,6 +119,12 @@
         return carry
 
     lax.fori_loop(1, T + 1, invite, 0)
+    for dd in range(1, D):
+        @pl.when(d >= dd)
+        def _():
+            pl.semaphore_signal(
+                go_q.at[dd - 1], inc=1, device_id={"desc": d - dd}, device_id_type=MESH
+            )
 
     def move(s, c):
         return pltpu.make_async_remote_copy(
@@ -143,11 +161,22 @@
         return carry
 
     lax.fori_loop(1, T + 1, move_down, 0)
-    for dd in range(1, D):
-        query_copy(dd, 0).start()
     for hh in range(1, H):
         query_copy(0, hh).start()
+    for dd in range(1, D):
+        @pl.when(d + dd < D)
+        def _():
+            pl.semaphore_wait(go_q.at[dd - 1], 1)
+
+        query_copy(dd, 0).start()
+
+    def widen(rows):
+        wide = q[rows, :].astype(jnp.float32)
+        q2[rows, :] = (wide * -2.0).astype(jnp.bfloat16)
+        sn[rows, :] = jnp.broadcast_to(jnp.sum(wide * wide, axis=1, keepdims=True), (R, 128))
+
     q[mine_rows, :] = x_ref[...]
+    widen(mine_rows)
 
     def move_up(s, carry):
         @pl.when(visiting(s) & (host_of(s) > i))
@@ -160,21 +189,21 @@
 
     lax.fori_loop(1, T + 1, move_up, 0)
 
+    def from_peer(dd, hh):
+        return rows_of(lax.rem(d + D - dd, D), lax.rem(h + H - hh, H))
+
+    for hh in range(1, H):
+        query_copy(0, hh).wait_recv()
+        widen(from_peer(0, hh))
     for dd in range(1, D):
         query_copy(dd, 0).wait_recv()
         for hh in range(1, H):
             query_relay(dd, hh).start()
-    for dd in range(D):
+        widen(from_peer(dd, 0))
+    for dd in range(1, D):
         for hh in range(1, H):
             query_copy(dd, hh).wait_recv()
-
-    def widen(t, carry):
-        rows = pl.ds(pl.multiple_of(t * TQ, TQ), TQ)
-        wide = q[rows, :].astype(jnp.float32)
-        sn[rows, :] = jnp.broadcast_to(jnp.sum(wide * wide, axis=1, keepdims=True), (TQ, 128))
-        return carry
-
-    lax.fori_loop(0, Q // TQ, widen, 0)
+            widen(from_peer(dd, hh))
 
     def result_copy(s, dd, hh):
         return pltpu.make_async_remote_copy(
@@ -190,52 +219,76 @@
             device_id={"blk": guest_of(s), "half": lax.rem(h + hh, H)}, device_id_type=MESH,
         )
 
-    def step_of(u):
-        return jnp.where(2 * i < n, T - u, u + 1)
-
     inf = functools.partial(jnp.full, fill_value=jnp.inf, dtype=jnp.float32)
 
-    def work(u, carry):
-        s = step_of(u)
+    def host_side(s, c):
+        piece = buf[s - 1, chunk(c), :]
+        wide = piece.astype(jnp.float32)
+        norms = jnp.broadcast_to(jnp.sum(wide * wide, axis=1, keepdims=True), (CR, 128))
+        for t in range(Q // TQ):
+            lanes = slice(t * TQ, (t + 1) * TQ)
+            lo, se = low[s - 1, :, lanes], sec[s - 1, :, lanes]
+            lo, se = fold(nt_dot(piece, q2[lanes, :]), norms, lo, se)
+            low[s - 1, :, lanes] = lo
+            sec[s - 1, :, lanes] = se
+
+    def host_send(s):
+        for t in range(D):
+            lanes = slice(t * share, (t + 1) * share)
+            lo, se = across_rows(low[s - 1, :, lanes], sec[s - 1, :, lanes])
+            mine[s - 1, t, 0:1, :] = lo
+            mine[s - 1, t, 1:2, :] = se
+        for dd, hh in reversed(others):
+            result_copy(s, dd, hh).start()
+
+    def guest_side(s, c):
+        piece = buf[s - 1, chunk(c), :]
+        lo, se = inf((8, CR)), inf((8, CR))
+        for t in range(Q // TQ):
+            rows = slice(t * TQ, (t + 1) * TQ)
+            lo, se = fold(nt_dot(q2[rows, :], piece), sn[rows, :], lo, se)
+        lo, se = across_rows(lo, se)
+        turned[s - 1, c, 0:1, :] = lo
+        turned[s - 1, c, 1:2, :] = se
+
+    def guest_send(s):
+        for hh in range(H):
+            return_copy(s, hh).start()
+
+    def meet(k, carry):
+        s, c = k // CH + 1, lax.rem(k, CH)
 
         @pl.when(hosting(s))
         def _():
-            low[...] = inf(low.shape)
-            sec[...] = inf(sec.shape)
-
-            def part_of(c, carry):
-                move(s, c).wait_recv()
-                wide = buf[s - 1, chunk(c), :].astype(jnp.float32)
-                norms = jnp.sum(wide * wide, axis=1, keepdims=True)
-                scaled = (wide * -2.0).astype(jnp.bfloat16)
-                for t in range(Q // TQ):
-                    lanes = slice(t * TQ, (t + 1) * TQ)
-                    lo, se = fold(nt_dot(scaled, q[lanes, :]) + norms, low[:, lanes], sec[:, lanes])
-                    low[:, lanes] = lo
-                    sec[:, lanes] = se
-                lo, se = inf((8, CR)), inf((8, CR))
-                for t in range(Q // TQ):
-                    rows = slice(t * TQ, (t + 1) * TQ)
-                    lo, se = fold(nt_dot(q[rows, :], scaled) + sn[rows, 0:1], lo, se)
-                lo, se = across_rows(lo, se)
-                turned[s - 1, c, 0:1, :] = lo
-                turned[s - 1, c, 1:2, :] = se
-                return carry
-
-            lax.fori_loop(0, CH, part_of, 0)
-            for t in range(D):
-                lanes = slice(t * share, (t + 1) * share)
-                lo, se = across_rows(low[:, lanes], sec[:, lanes])
-                mine[s - 1, t, 0:1, :] = lo
-                mine[s - 1, t, 1:2, :] = se
-            for dd, hh in reversed(others):
-                result_copy(s, dd, hh).start()
-            for hh in range(H):
-                return_copy(s, hh).start()
-
-        return carry
-
-    lax.fori_loop(0, T, work, 0)
+            move(s, c).wait_recv()
+
+            @pl.when(c < CH - 1)
+            def _():
+                host_side(s, c)
+                guest_side(s, c)
+
+            @pl.when(c == CH - 1)
+            def _():
+                def side(turn, carry):
+                    @pl.when((turn == 0) == (2 * i < n))
+                    def _():
+                        host_side(s, c)
+                        host_send(s)
+
+                    @pl.when((turn == 0) != (2 * i < n))
+                    def _():
+                        guest_side(s, c)
+                        guest_send(s)
+
+                    return carry
+
+                lax.fori_loop(0, 2, side, 0)
+
+        return carry
+
+    low[...] = inf(low.shape)
+    sec[...] = inf(sec.shape)
+    lax.fori_loop(0, T * CH, meet, 0)
 
     own = q[pl.ds(pl.multiple_of(d * share, share), share), :].astype(jnp.float32)
     square = own * own
@@ -260,9 +313,7 @@
     for hh in range(1, H):
         query_copy(0, hh).wait_send()
 
-    def finish(u, carry):
-        s = step_of(u)
-
+    def finish(s, carry):
         @pl.when(visiting(s))
         def _():
             for hh in range(H):
@@ -286,7 +337,7 @@
 
         return carry
 
-    lax.fori_loop(0, T, finish, 0)
+    lax.fori_loop(1, T + 1, finish, 0)
 
     def sent_results(s, carry):
         @pl.when(hosting(s))
@@ -322,15 +373,17 @@
                 pltpu.VMEM((R, depth), jnp.bfloat16),
                 pltpu.VMEM((T, R, depth), jnp.bfloat16),
                 pltpu.VMEM((D * share, depth), jnp.bfloat16),
+                pltpu.VMEM((D * share, depth), jnp.bfloat16),
                 pltpu.VMEM((D * share, 128), jnp.float32),
-                pltpu.VMEM((8, D * share), jnp.float32),
-                pltpu.VMEM((8, D * share), jnp.float32),
+                pltpu.VMEM((T, 8, D * share), jnp.float32),
+                pltpu.VMEM((T, 8, D * share), jnp.float32),
                 pltpu.VMEM((T, D, 2, share), jnp.float32),
                 pltpu.VMEM((T, D * H, 2, share), jnp.float32),
                 pltpu.VMEM((T, CH, 2, CR), jnp.float32),
                 pltpu.VMEM((T, H, CH, 2, CR), jnp.float32),
                 pltpu.SemaphoreType.DMA,
                 pltpu.SemaphoreType.REGULAR((T,)),
+                pltpu.SemaphoreType.REGULAR((max(D - 1, 1),)),
                 pltpu.SemaphoreType.DMA((T, CH)),
                 pltpu.SemaphoreType.DMA((T, CH)),
                 pltpu.SemaphoreType.DMA((D * H,)),

time: 19.1 us -> 17 us (0.89)
  Pallas kernels: 17.6 us -> 15.6 us
    pallas_call x1, Pallas kernels: 17.6 us -> 15.6 us  [per_device(): pl.pallas_call(functools.partial(kernel, n, D, H, CH), out_shape=(out, ou...]
where the time goes in v2:
time: 17 us; the launch traced here: 16.9 us
  Pallas kernels  15.6 us (92%)
  between operations  0.64 us (4%)
  other arithmetic  0.63 us (4%)
    pallas_call x1, Pallas kernels, per_device(): pl.pallas_call(functools.partial(kernel, n, D, H, CH), out_shape=(out, ou...  15.6 us
    add x1, other arithmetic, per_device(): return (norms + lo, norms + se)  0.63 us

profile of v2, /device:TPU:0, one launch (start us, length us, event | category | flops | bytes accessed | tf_op | source)
XLA Modules:
  0.0 16.9 jit_solution(4428710176765152216)
XLA Ops:
  0.6 15.6 %shard_map.30 = (f32[3,1,1024]{2,1,0:T(1,128)S(1)}, f32[3,1,1024]{2,1,0:T(1,128)S(1)}, f32[1,1024]{1,0:T(1,128)S(1)}) custom-call(bf16[512,128]{1,0:T(8,128)(2,1)} %bitcast.3), custom_call_target="tpu_custom_call" | custom-call | tf_op jit(solution)/shard_map/pallas_call | solution.py:367
  16.2 0.6 %broadcast_add_fusion = (f32[3,1,1024]{2,1,0:T(1,128)}, f32[3,1,1024]{2,1,0:T(1,128)}) fusion(f32[3,1,1024]{2,1,0:T(1,128)S(1)} %get-tuple-element.7, f32[1024]{0:T(1024)S(1)} %bitcast.2, f32[3,1,1024]{2,1,0:T(1,128)S(1)} %get-tuple-element.6), kind=kLoop, calls=%fused_computation | loop fusion | flops 6144 | bytes 53248 | tf_op jit(solution)/shard_map/add | solution.py:398

commit v3 on v2

--- a/solution.py
+++ b/solution.py
@@ -46,7 +46,7 @@
 def kernel(
     n, D, H, CH, x_hbm, best_ref, second_ref, norm_ref,
     x_ref, buf, q, q2, sn, low, sec, mine, inbox, turned, returned,
-    x_sem, go, go_q, z_send, z_recv, q_send, q_recv, p_send, p_recv, m_send, m_recv,
+    x_sem, go, go_q, z_send, z_recv, y_send, y_recv, q_send, q_recv, p_send, p_recv, m_send, m_recv,
 ):
     R = x_hbm.shape[0]
     load = pltpu.make_async_copy(x_hbm, x_ref, x_sem)
@@ -59,6 +59,7 @@
     i = lax.axis_index("blk")
     d = lax.axis_index("desc")
     h = lax.axis_index("half")
+    inf = functools.partial(jnp.full, fill_value=jnp.inf, dtype=jnp.float32)
     others = [(dd, hh) for dd in range(D) for hh in range(H) if (dd, hh) != (0, 0)]
 
     if n % 2 == 0:
@@ -126,6 +127,15 @@
                 go_q.at[dd - 1], inc=1, device_id={"desc": d - dd}, device_id_type=MESH
             )
 
+    detour = n % 2 == 0 and D > 1 and H > 1 and CH == 2
+    gains = (i == 0) & (d == 0) & (h == H - 1) if detour else i < 0
+
+    def keeps(s, c, guest):
+        if not detour:
+            return i >= 0
+        elsewhere = (d != 1) | (h != 0) | (i != (T if guest else 0))
+        return (s != T) | (c != CH - 1) | elsewhere
+
     def move(s, c):
         return pltpu.make_async_remote_copy(
             src_ref=x_ref.at[chunk(c)], dst_ref=buf.at[s - 1, chunk(c)],
@@ -135,40 +145,52 @@
 
     mine_rows = rows_of(d, h)
 
-    def query_copy(dd, hh):
-        return pltpu.make_async_remote_copy(
-            src_ref=x_ref, dst_ref=q.at[mine_rows],
-            send_sem=q_send.at[dd * H + hh], recv_sem=q_recv.at[dd * H + hh],
+    def part_of(d_at, h_at, c):
+        return pl.ds(pl.multiple_of((d_at * H + h_at) * R + c * CR, CR), CR)
+
+    def query_copy(dd, hh, c):
+        return pltpu.make_async_remote_copy(
+            src_ref=x_ref.at[chunk(c)], dst_ref=q.at[part_of(d, h, c)],
+            send_sem=q_send.at[dd * H + hh, c], recv_sem=q_recv.at[dd * H + hh, c],
             device_id=peer(dd, hh), device_id_type=MESH,
         )
 
-    def query_relay(dd, hh):
-        src_rows = rows_of(lax.rem(d + D - dd, D), h)
-        return pltpu.make_async_remote_copy(
-            src_ref=q.at[src_rows], dst_ref=q.at[src_rows],
-            send_sem=q_send.at[dd * H + hh], recv_sem=q_recv.at[dd * H + hh],
+    def query_relay(dd, hh, c):
+        rows = part_of(lax.rem(d + D - dd, D), h, c)
+        return pltpu.make_async_remote_copy(
+            src_ref=q.at[rows], dst_ref=q.at[rows],
+            send_sem=q_send.at[dd * H + hh, c], recv_sem=q_recv.at[dd * H + hh, c],
             device_id=peer(0, hh), device_id_type=MESH,
         )
 
+    def detour_copy():
+        return pltpu.make_async_remote_copy(
+            src_ref=q.at[part_of(1, 0, CH - 1)], dst_ref=buf.at[T, chunk(0)],
+            send_sem=y_send, recv_sem=y_recv,
+            device_id={"blk": i - T, "half": H - 1}, device_id_type=MESH,
+        )
+
     load.wait()
 
     def move_down(s, carry):
-        @pl.when(visiting(s) & (host_of(s) < i))
-        def _():
-            for c in range(CH):
+        for c in range(CH):
+            @pl.when(visiting(s) & (host_of(s) < i) & keeps(s, c, True))
+            def _():
                 move(s, c).start()
 
         return carry
 
     lax.fori_loop(1, T + 1, move_down, 0)
     for hh in range(1, H):
-        query_copy(0, hh).start()
+        for c in range(CH):
+            query_copy(0, hh, c).start()
     for dd in range(1, D):
         @pl.when(d + dd < D)
         def _():
             pl.semaphore_wait(go_q.at[dd - 1], 1)
 
-        query_copy(dd, 0).start()
+        for c in reversed(range(CH)):
+            query_copy(dd, 0, c).start()
 
     def widen(rows):
         wide = q[rows, :].astype(jnp.float32)
@@ -193,16 +215,31 @@
         return rows_of(lax.rem(d + D - dd, D), lax.rem(h + H - hh, H))
 
     for hh in range(1, H):
-        query_copy(0, hh).wait_recv()
+        for c in range(CH):
+            query_copy(0, hh, c).wait_recv()
         widen(from_peer(0, hh))
+    own = q[pl.ds(pl.multiple_of(d * share, share), share), :].astype(jnp.float32)
+    square = own * own
+    head = square.astype(jnp.bfloat16)
+    tail = (square - head.astype(jnp.float32)).astype(jnp.bfloat16)
+    ones = jnp.ones((8, q.shape[1]), jnp.bfloat16)
+    norm_ref[...] = (nt_dot(ones, head) + nt_dot(ones, tail))[0:1]
+    low[...] = inf(low.shape)
+    sec[...] = inf(sec.shape)
     for dd in range(1, D):
-        query_copy(dd, 0).wait_recv()
-        for hh in range(1, H):
-            query_relay(dd, hh).start()
+        for c in reversed(range(CH)):
+            query_copy(dd, 0, c).wait_recv()
+            if detour and c == CH - 1 and dd == D - 1:
+                @pl.when((i == T) & (d == 0) & (h == 0))
+                def _():
+                    detour_copy().start()
+            for hh in range(1, H):
+                query_relay(dd, hh, c).start()
         widen(from_peer(dd, 0))
     for dd in range(1, D):
         for hh in range(1, H):
-            query_copy(dd, hh).wait_recv()
+            for c in range(CH):
+                query_copy(dd, hh, c).wait_recv()
             widen(from_peer(dd, hh))
 
     def result_copy(s, dd, hh):
@@ -212,17 +249,23 @@
             device_id=peer(dd, hh), device_id_type=MESH,
         )
 
-    def return_copy(s, hh):
-        return pltpu.make_async_remote_copy(
-            src_ref=turned.at[s - 1], dst_ref=returned.at[s - 1, hh],
-            send_sem=m_send.at[s - 1, hh], recv_sem=m_recv.at[s - 1, hh],
+    def return_copy(s, hh, c):
+        return pltpu.make_async_remote_copy(
+            src_ref=turned.at[s - 1, c], dst_ref=returned.at[s - 1, hh, c],
+            send_sem=m_send.at[s - 1, hh, c], recv_sem=m_recv.at[s - 1, hh, c],
             device_id={"blk": guest_of(s), "half": lax.rem(h + hh, H)}, device_id_type=MESH,
         )
 
-    inf = functools.partial(jnp.full, fill_value=jnp.inf, dtype=jnp.float32)
-
-    def host_side(s, c):
-        piece = buf[s - 1, chunk(c), :]
+    def detour_return(hh):
+        return pltpu.make_async_remote_copy(
+            src_ref=turned.at[T, 0], dst_ref=returned.at[T - 1, hh, CH - 1],
+            send_sem=m_send.at[T, hh, 0], recv_sem=m_recv.at[T - 1, hh, CH - 1],
+            device_id={"blk": i + T, "desc": 1, "half": hh},
+            device_id_type=MESH,
+        )
+
+    def host_side(s, at, c):
+        piece = buf[at, chunk(c), :]
         wide = piece.astype(jnp.float32)
         norms = jnp.broadcast_to(jnp.sum(wide * wide, axis=1, keepdims=True), (CR, 128))
         for t in range(Q // TQ):
@@ -241,83 +284,134 @@
         for dd, hh in reversed(others):
             result_copy(s, dd, hh).start()
 
-    def guest_side(s, c):
-        piece = buf[s - 1, chunk(c), :]
-        lo, se = inf((8, CR)), inf((8, CR))
+    def guest_side(at, rows, width):
+        piece = buf[at, rows, :]
+        lo, se = inf((8, width)), inf((8, width))
         for t in range(Q // TQ):
             rows = slice(t * TQ, (t + 1) * TQ)
             lo, se = fold(nt_dot(q2[rows, :], piece), sn[rows, :], lo, se)
-        lo, se = across_rows(lo, se)
-        turned[s - 1, c, 0:1, :] = lo
-        turned[s - 1, c, 1:2, :] = se
-
-    def guest_send(s):
-        for hh in range(H):
-            return_copy(s, hh).start()
+        return across_rows(lo, se)
+
+    def guest_chunk(s, at, c):
+        lo, se = guest_side(at, chunk(c), CR)
+        turned[at, c, 0:1, :] = lo
+        turned[at, c, 1:2, :] = se
+
+        @pl.when(at < T)
+        def _():
+            for hh in range(H):
+                return_copy(s, hh, c).start()
+
+        if detour:
+            @pl.when(at == T)
+            def _():
+                for hh in range(H):
+                    detour_return(hh).start()
+
+    def guest_whole(s):
+        lo, se = guest_side(s - 1, slice(0, R), R)
+        for c in range(CH):
+            lanes = slice(c * CR, (c + 1) * CR)
+            turned[s - 1, c, 0:1, :] = lo[:, lanes]
+            turned[s - 1, c, 1:2, :] = se[:, lanes]
+            for hh in range(H):
+                return_copy(s, hh, c).start()
+
+    def turn_of(k):
+        rest = (T - 1) * CH
+        upper = (2 * i >= n) & (k > 0)
+        far = upper & (k <= rest)
+        s = jnp.where(upper, jnp.where(far, 1 + (k + CH - 1) // CH, 1), k // CH + 1)
+        c = jnp.where(upper, jnp.where(far, lax.rem(k + CH - 1, CH), k - rest), lax.rem(k, CH))
+        return s, c
+
+    items = T * CH + (1 if detour else 0)
 
     def meet(k, carry):
-        s, c = k // CH + 1, lax.rem(k, CH)
-
-        @pl.when(hosting(s))
+        s, c = turn_of(k)
+        at = s - 1
+        comes = hosting(s) & keeps(s, c, False)
+        closes = (c == CH - 1) & jnp.logical_not(gains & (s == T))
+        lost, extra = i < 0, i < 0
+        if detour:
+            extra = k == T * CH
+            s, c, at = jnp.where(extra, T, s), jnp.where(extra, 0, c), jnp.where(extra, T, at)
+            comes = jnp.where(extra, gains, comes)
+            lost = jnp.logical_not(keeps(s, CH - 1, False))
+            closes = extra | closes | (lost & (c == CH - 2))
+
+        @pl.when(comes & (at < T))
         def _():
             move(s, c).wait_recv()
 
-            @pl.when(c < CH - 1)
-            def _():
-                host_side(s, c)
-                guest_side(s, c)
-
-            @pl.when(c == CH - 1)
-            def _():
-                def side(turn, carry):
-                    @pl.when((turn == 0) == (2 * i < n))
-                    def _():
-                        host_side(s, c)
-                        host_send(s)
-
-                    @pl.when((turn == 0) != (2 * i < n))
-                    def _():
-                        guest_side(s, c)
-                        guest_send(s)
-
-                    return carry
-
-                lax.fori_loop(0, 2, side, 0)
-
-        return carry
-
-    low[...] = inf(low.shape)
-    sec[...] = inf(sec.shape)
-    lax.fori_loop(0, T * CH, meet, 0)
-
-    own = q[pl.ds(pl.multiple_of(d * share, share), share), :].astype(jnp.float32)
-    square = own * own
-    head = square.astype(jnp.bfloat16)
-    tail = (square - head.astype(jnp.float32)).astype(jnp.bfloat16)
-    ones = jnp.ones((8, q.shape[1]), jnp.bfloat16)
-    norm_ref[...] = (nt_dot(ones, head) + nt_dot(ones, tail))[0:1]
+        if detour:
+            @pl.when(comes & (at == T))
+            def _():
+                detour_copy().wait_recv()
+
+        lower = 2 * i < n
+        both = comes & jnp.logical_not(closes) & jnp.logical_not(lower)
+
+        @pl.when(both)
+        def _():
+            host_side(s, at, c)
+            guest_chunk(s, at, c)
+
+        def side(turn, carry):
+            host_turn = (turn == 0) == (lower | (s != T))
+
+            @pl.when(host_turn & comes)
+            def _():
+                host_side(s, at, c)
+
+                @pl.when(closes)
+                def _():
+                    host_send(s)
+
+            guest_turn = jnp.logical_not(host_turn) & comes & closes
+
+            @pl.when(guest_turn & lower & (extra | jnp.logical_not(lost)))
+            def _():
+                guest_whole(s)
+
+            @pl.when(guest_turn & (jnp.logical_not(lower) | lost | extra))
+            def _():
+                guest_chunk(s, at, c)
+
+            return carry
+
+        lax.fori_loop(0, jnp.where(both, 0, 2), side, 0)
+        return carry
+
+    lax.fori_loop(0, items, meet, 0)
 
     def sent(s, carry):
-        @pl.when(visiting(s))
-        def _():
-            for c in range(CH):
+        for c in range(CH):
+            @pl.when(visiting(s) & keeps(s, c, True))
+            def _():
                 move(s, c).wait_send()
 
         return carry
 
     lax.fori_loop(1, T + 1, sent, 0)
-    for dd in range(1, D):
-        query_copy(dd, 0).wait_send()
+    if detour:
+        @pl.when((i == T) & (d == 0) & (h == 0))
+        def _():
+            detour_copy().wait_send()
+    for c in range(CH):
+        for dd in range(1, D):
+            query_copy(dd, 0, c).wait_send()
+            for hh in range(1, H):
+                query_relay(dd, hh, c).wait_send()
         for hh in range(1, H):
-            query_relay(dd, hh).wait_send()
-    for hh in range(1, H):
-        query_copy(0, hh).wait_send()
+            query_copy(0, hh, c).wait_send()
 
     def finish(s, carry):
         @pl.when(visiting(s))
         def _():
             for hh in range(H):
-                return_copy(s, hh).wait_recv()
+                for c in range(CH):
+                    return_copy(s, hh, c).wait_recv()
             for hh in range(H):
                 for c in range(CH):
                     at = lax.rem(h + H - hh, H) * CH + c
@@ -344,12 +438,21 @@
         def _():
             for dd, hh in others:
                 result_copy(s, dd, hh).wait_send()
+
+        for c in range(CH):
+            @pl.when(hosting(s) & keeps(s, c, False))
+            def _():
+                for hh in range(H):
+                    return_copy(s, hh, c).wait_send()
+
+        return carry
+
+    lax.fori_loop(1, T + 1, sent_results, 0)
+    if detour:
+        @pl.when(gains)
+        def _():
             for hh in range(H):
-                return_copy(s, hh).wait_send()
-
-        return carry
-
-    lax.fori_loop(1, T + 1, sent_results, 0)
+                detour_return(hh).wait_send()
 
 
 def solution(mesh):
@@ -371,7 +474,7 @@
             out_specs=(vmem, vmem, vmem),
             scratch_shapes=[
                 pltpu.VMEM((R, depth), jnp.bfloat16),
-                pltpu.VMEM((T, R, depth), jnp.bfloat16),
+                pltpu.VMEM((T + 1, R, depth), jnp.bfloat16),
                 pltpu.VMEM((D * share, depth), jnp.bfloat16),
                 pltpu.VMEM((D * share, depth), jnp.bfloat16),
                 pltpu.VMEM((D * share, 128), jnp.float32),
@@ -379,19 +482,21 @@
                 pltpu.VMEM((T, 8, D * share), jnp.float32),
                 pltpu.VMEM((T, D, 2, share), jnp.float32),
                 pltpu.VMEM((T, D * H, 2, share), jnp.float32),
-                pltpu.VMEM((T, CH, 2, CR), jnp.float32),
+                pltpu.VMEM((T + 1, CH, 2, CR), jnp.float32),
                 pltpu.VMEM((T, H, CH, 2, CR), jnp.float32),
                 pltpu.SemaphoreType.DMA,
                 pltpu.SemaphoreType.REGULAR((T,)),
                 pltpu.SemaphoreType.REGULAR((max(D - 1, 1),)),
                 pltpu.SemaphoreType.DMA((T, CH)),
                 pltpu.SemaphoreType.DMA((T, CH)),
-                pltpu.SemaphoreType.DMA((D * H,)),
-                pltpu.SemaphoreType.DMA((D * H,)),
+                pltpu.SemaphoreType.DMA,
+                pltpu.SemaphoreType.DMA,
+                pltpu.SemaphoreType.DMA((D * H, CH)),
+                pltpu.SemaphoreType.DMA((D * H, CH)),
                 pltpu.SemaphoreType.DMA((T, D * H)),
                 pltpu.SemaphoreType.DMA((T, D * H)),
-                pltpu.SemaphoreType.DMA((T, H)),
-                pltpu.SemaphoreType.DMA((T, H)),
+                pltpu.SemaphoreType.DMA((T + 1, H, CH)),
+                pltpu.SemaphoreType.DMA((T, H, CH)),
             ],
             compiler_params=pltpu.CompilerParams(collective_id=0, has_side_effects=True),
         )(block)

time: 17 us -> 16.7 us (0.982)
  Pallas kernels: 15.6 us -> 15.3 us
    pallas_call x1, Pallas kernels: 15.6 us -> 15.3 us  [per_device(): pl.pallas_call(functools.partial(kernel, n, D, H, CH), out_shape=(out, ou...]
where the time goes in v3:
time: 16.7 us; the launch traced here: 16.6 us
  Pallas kernels  15.3 us (92%)
  between operations  0.64 us (4%)
  other arithmetic  0.63 us (4%)
    pallas_call x1, Pallas kernels, per_device(): pl.pallas_call(functools.partial(kernel, n, D, H, CH), out_shape=(out, ou...  15.3 us
    add x1, other arithmetic, per_device(): return (norms + lo, norms + se)  0.63 us

profile of v3, /device:TPU:0, one launch (start us, length us, event | category | flops | bytes accessed | tf_op | source)
XLA Modules:
  0.0 16.6 jit_solution(5820637402147887309)
XLA Ops:
  0.6 15.3 %shard_map.30 = (f32[3,1,1024]{2,1,0:T(1,128)S(1)}, f32[3,1,1024]{2,1,0:T(1,128)S(1)}, f32[1,1024]{1,0:T(1,128)S(1)}) custom-call(bf16[512,128]{1,0:T(8,128)(2,1)} %bitcast.3), custom_call_target="tpu_custom_call" | custom-call | tf_op jit(solution)/shard_map/pallas_call | solution.py:470
  16.0 0.6 %broadcast_add_fusion = (f32[3,1,1024]{2,1,0:T(1,128)}, f32[3,1,1024]{2,1,0:T(1,128)}) fusion(f32[3,1,1024]{2,1,0:T(1,128)S(1)} %get-tuple-element.7, f32[1024]{0:T(1024)S(1)} %bitcast.2, f32[3,1,1024]{2,1,0:T(1,128)S(1)} %get-tuple-element.6), kind=kLoop, calls=%fused_computation | loop fusion | flops 6144 | bytes 53248 | tf_op jit(solution)/shard_map/add | solution.py:503

commit v4 on v3

--- a/solution.py
+++ b/solution.py
@@ -350,40 +350,46 @@
                 detour_copy().wait_recv()
 
         lower = 2 * i < n
-        both = comes & jnp.logical_not(closes) & jnp.logical_not(lower)
-
-        @pl.when(both)
+
+        @pl.when(comes & jnp.logical_not(lower))
         def _():
             host_side(s, at, c)
             guest_chunk(s, at, c)
 
-        def side(turn, carry):
-            host_turn = (turn == 0) == (lower | (s != T))
-
-            @pl.when(host_turn & comes)
-            def _():
-                host_side(s, at, c)
-
-                @pl.when(closes)
-                def _():
-                    host_send(s)
-
-            guest_turn = jnp.logical_not(host_turn) & comes & closes
-
-            @pl.when(guest_turn & lower & (extra | jnp.logical_not(lost)))
+            @pl.when(closes)
+            def _():
+                host_send(s)
+
+        @pl.when(comes & lower)
+        def _():
+            host_side(s, at, c)
+
+            @pl.when(closes)
+            def _():
+                host_send(s)
+
+            whole = closes & (extra | jnp.logical_not(lost))
+
+            @pl.when(whole & ((d == 0) | (s == T)))
             def _():
                 guest_whole(s)
 
-            @pl.when(guest_turn & (jnp.logical_not(lower) | lost | extra))
+            @pl.when(extra | (closes & lost))
             def _():
                 guest_chunk(s, at, c)
 
-            return carry
-
-        lax.fori_loop(0, jnp.where(both, 0, 2), side, 0)
         return carry
 
     lax.fori_loop(0, items, meet, 0)
+
+    def put_off(s, carry):
+        @pl.when((2 * i < n) & (d > 0) & hosting(s))
+        def _():
+            guest_whole(s)
+
+        return carry
+
+    lax.fori_loop(1, T, put_off, 0)
 
     def sent(s, carry):
         for c in range(CH):

time: 16.7 us -> 16.3 us (0.976)
  Pallas kernels: 15.3 us -> 14.9 us
    pallas_call x1, Pallas kernels: 15.3 us -> 14.9 us  [per_device(): pl.pallas_call(functools.partial(kernel, n, D, H, CH), out_shape=(out, ou...]
where the time goes in v4:
time: 16.3 us; the launch traced here: 16.2 us
  Pallas kernels  14.9 us (91%)
  between operations  0.64 us (4%)
  other arithmetic  0.63 us (4%)
    pallas_call x1, Pallas kernels, per_device(): pl.pallas_call(functools.partial(kernel, n, D, H, CH), out_shape=(out, ou...  14.9 us
    add x1, other arithmetic, per_device(): return (norms + lo, norms + se)  0.63 us

profile of v4, /device:TPU:0, one launch (start us, length us, event | category | flops | bytes accessed | tf_op | source)
XLA Modules:
  0.0 16.2 jit_solution(13930582420920017741)
XLA Ops:
  0.6 14.9 %shard_map.30 = (f32[3,1,1024]{2,1,0:T(1,128)S(1)}, f32[3,1,1024]{2,1,0:T(1,128)S(1)}, f32[1,1024]{1,0:T(1,128)S(1)}) custom-call(bf16[512,128]{1,0:T(8,128)(2,1)} %bitcast.3), custom_call_target="tpu_custom_call" | custom-call | tf_op jit(solution)/shard_map/pallas_call | solution.py:476
  15.5 0.6 %broadcast_add_fusion = (f32[3,1,1024]{2,1,0:T(1,128)}, f32[3,1,1024]{2,1,0:T(1,128)}) fusion(f32[3,1,1024]{2,1,0:T(1,128)S(1)} %get-tuple-element.7, f32[1024]{0:T(1024)S(1)} %bitcast.2, f32[3,1,1024]{2,1,0:T(1,128)S(1)} %get-tuple-element.6), kind=kLoop, calls=%fused_computation | loop fusion | flops 6144 | bytes 53248 | tf_op jit(solution)/shard_map/add | solution.py:509

commit v5 on v4

--- a/solution.py
+++ b/solution.py
@@ -108,6 +108,16 @@
             pl.semaphore_signal(barrier, inc=1, device_id={"desc": d + dd}, device_id_type=MESH)
     for hh in range(1, H):
         pl.semaphore_signal(barrier, inc=1, device_id=peer(0, hh), device_id_type=MESH)
+    straight = D > 1 and H > 1
+    if straight:
+        for dd in range(1, D):
+            @pl.when((d + dd < D) & (h == H - 1))
+            def _():
+                pl.semaphore_signal(
+                    barrier, inc=1, device_id={"desc": d + dd, "half": 0}, device_id_type=MESH
+                )
+
+        met = met + jnp.where(h == 0, d, 0)
     pl.semaphore_wait(barrier, H - 1 + d + met)
 
     def invite(s, carry):
@@ -161,6 +171,14 @@
             src_ref=q.at[rows], dst_ref=q.at[rows],
             send_sem=q_send.at[dd * H + hh, c], recv_sem=q_recv.at[dd * H + hh, c],
             device_id=peer(0, hh), device_id_type=MESH,
+        )
+
+    def straight_copy(dd):
+        at = dd * H + H - 1
+        return pltpu.make_async_remote_copy(
+            src_ref=x_ref.at[chunk(0)], dst_ref=q.at[part_of(d, 0, 0)],
+            send_sem=q_send.at[at, 0], recv_sem=q_recv.at[at, 0],
+            device_id={"desc": lax.rem(d + dd, D), "half": H - 1}, device_id_type=MESH,
         )
 
     def detour_copy():
@@ -190,6 +208,11 @@
             pl.semaphore_wait(go_q.at[dd - 1], 1)
 
         for c in reversed(range(CH)):
+            if straight and c == 0:
+                @pl.when(h == 0)
+                def _():
+                    straight_copy(dd).start()
+
             query_copy(dd, 0, c).start()
 
     def widen(rows):
@@ -234,7 +257,12 @@
                 def _():
                     detour_copy().start()
             for hh in range(1, H):
-                query_relay(dd, hh, c).start()
+                if straight and (hh, c) == (H - 1, 0):
+                    @pl.when(h != 0)
+                    def _():
+                        query_relay(dd, hh, c).start()
+                else:
+                    query_relay(dd, hh, c).start()
         widen(from_peer(dd, 0))
     for dd in range(1, D):
         for hh in range(1, H):
@@ -274,6 +302,34 @@
             lo, se = fold(nt_dot(piece, q2[lanes, :]), norms, lo, se)
             low[s - 1, :, lanes] = lo
             sec[s - 1, :, lanes] = se
+
+    def host_close(s, at, c):
+        piece = buf[at, chunk(c), :]
+        wide = piece.astype(jnp.float32)
+        norms = jnp.broadcast_to(jnp.sum(wide * wide, axis=1, keepdims=True), (CR, 128))
+
+        def column(dd, carry):
+            t = lax.rem(d + dd, D)
+            for u in range(share // TQ):
+                lanes = pl.ds(pl.multiple_of(t * share + u * TQ, TQ), TQ)
+                lo, se = low[s - 1, :, lanes], sec[s - 1, :, lanes]
+                lo, se = across_rows(*fold(nt_dot(piece, q2[lanes, :]), norms, lo, se))
+                mine[s - 1, t, 0:1, u * TQ : (u + 1) * TQ] = lo
+                mine[s - 1, t, 1:2, u * TQ : (u + 1) * TQ] = se
+
+            @pl.when(dd < D)
+            def _():
+                for hh in range(H):
+                    result_copy(s, dd, hh).start()
+
+            @pl.when(dd == D)
+            def _():
+                for hh in range(1, H):
+                    result_copy(s, 0, hh).start()
+
+            return carry
+
+        lax.fori_loop(1, D + 1, column, 0)
 
     def host_send(s):
         for t in range(D):
@@ -351,7 +407,9 @@
 
         lower = 2 * i < n
 
-        @pl.when(comes & jnp.logical_not(lower))
+        last_far = closes & (s == T) & jnp.logical_not(lower) & (T > 1)
+
+        @pl.when(comes & jnp.logical_not(lower) & jnp.logical_not(last_far))
         def _():
             host_side(s, at, c)
             guest_chunk(s, at, c)
@@ -360,11 +418,23 @@
             def _():
                 host_send(s)
 
+        @pl.when(comes & last_far)
+        def _():
+            guest_chunk(s, at, c)
+
         @pl.when(comes & lower)
         def _():
-            host_side(s, at, c)
-
-            @pl.when(closes)
+            travels = closes & (d > 0)
+
+            @pl.when(travels)
+            def _():
+                host_close(s, at, c)
+
+            @pl.when(jnp.logical_not(travels))
+            def _():
+                host_side(s, at, c)
+
+            @pl.when(closes & jnp.logical_not(travels))
             def _():
                 host_send(s)
 
@@ -381,6 +451,12 @@
         return carry
 
     lax.fori_loop(0, items, meet, 0)
+
+    if T > 1:
+        @pl.when((2 * i >= n) & hosting(T))
+        def _():
+            host_side(T, T - 1, CH - 1)
+            host_send(T)
 
     def put_off(s, carry):
         @pl.when((2 * i < n) & (d > 0) & hosting(s))
@@ -411,6 +487,27 @@
                 query_relay(dd, hh, c).wait_send()
         for hh in range(1, H):
             query_copy(0, hh, c).wait_send()
+
+    def sent_results(s, carry):
+        @pl.when(hosting(s))
+        def _():
+            for dd, hh in others:
+                result_copy(s, dd, hh).wait_send()
+
+        for c in range(CH):
+            @pl.when(hosting(s) & keeps(s, c, False))
+            def _():
+                for hh in range(H):
+                    return_copy(s, hh, c).wait_send()
+
+        return carry
+
+    lax.fori_loop(1, T + 1, sent_results, 0)
+    if detour:
+        @pl.when(gains)
+        def _():
+            for hh in range(H):
+                detour_return(hh).wait_send()
 
     def finish(s, carry):
         @pl.when(visiting(s))
@@ -438,27 +535,6 @@
         return carry
 
     lax.fori_loop(1, T + 1, finish, 0)
-
-    def sent_results(s, carry):
-        @pl.when(hosting(s))
-        def _():
-            for dd, hh in others:
-                result_copy(s, dd, hh).wait_send()
-
-        for c in range(CH):
-            @pl.when(hosting(s) & keeps(s, c, False))
-            def _():
-                for hh in range(H):
-                    return_copy(s, hh, c).wait_send()
-
-        return carry
-
-    lax.fori_loop(1, T + 1, sent_results, 0)
-    if detour:
-        @pl.when(gains)
-        def _():
-            for hh in range(H):
-                detour_return(hh).wait_send()
 
 
 def solution(mesh):

time: 16.3 us -> 16.2 us (level)
  Pallas kernels: 14.9 us -> 14.7 us
    pallas_call x1, Pallas kernels: 14.9 us -> 14.7 us  [per_device(): pl.pallas_call(functools.partial(kernel, n, D, H, CH), out_shape=(out, ou...]
where the time goes in v5:
time: 16.2 us; the launch traced here: 16 us
  Pallas kernels  14.7 us (91%)
  between operations  0.64 us (4%)
  other arithmetic  0.63 us (4%)
    pallas_call x1, Pallas kernels, per_device(): pl.pallas_call(functools.partial(kernel, n, D, H, CH), out_shape=(out, ou...  14.7 us
    add x1, other arithmetic, per_device(): return (norms + lo, norms + se)  0.63 us

profile of v5, /device:TPU:0, one launch (start us, length us, event | category | flops | bytes accessed | tf_op | source)
XLA Modules:
  0.0 16.0 jit_solution(17608932853155146041)
XLA Ops:
  0.6 14.7 %shard_map.30 = (f32[3,1,1024]{2,1,0:T(1,128)S(1)}, f32[3,1,1024]{2,1,0:T(1,128)S(1)}, f32[1,1024]{1,0:T(1,128)S(1)}) custom-call(bf16[512,128]{1,0:T(8,128)(2,1)} %bitcast.3), custom_call_target="tpu_custom_call" | custom-call | tf_op jit(solution)/shard_map/pallas_call | solution.py:552
  15.4 0.6 %broadcast_add_fusion = (f32[3,1,1024]{2,1,0:T(1,128)}, f32[3,1,1024]{2,1,0:T(1,128)}) fusion(f32[3,1,1024]{2,1,0:T(1,128)S(1)} %get-tuple-element.7, f32[1024]{0:T(1024)S(1)} %bitcast.2, f32[3,1,1024]{2,1,0:T(1,128)S(1)} %get-tuple-element.6), kind=kLoop, calls=%fused_computation | loop fusion | flops 6144 | bytes 53248 | tf_op jit(solution)/shard_map/add | solution.py:585

commit v6 on v5

--- a/solution.py
+++ b/solution.py
@@ -190,9 +190,14 @@
 
     load.wait()
 
-    def move_down(s, carry):
+    yields = (i == T) & (d == 1) & (h == H - 1) if detour else i < 0
+
+    def move_down(s, carry, again=False):
         for c in range(CH):
-            @pl.when(visiting(s) & (host_of(s) < i) & keeps(s, c, True))
+            now = yields & (c == CH - 1)
+            now = now if again else jnp.logical_not(now)
+
+            @pl.when(now & visiting(s) & (host_of(s) < i) & keeps(s, c, True))
             def _():
                 move(s, c).start()
 
@@ -240,6 +245,8 @@
     for hh in range(1, H):
         for c in range(CH):
             query_copy(0, hh, c).wait_recv()
+        if hh == 1:
+            lax.fori_loop(1, T + 1, functools.partial(move_down, again=True), 0)
         widen(from_peer(0, hh))
     own = q[pl.ds(pl.multiple_of(d * share, share), share), :].astype(jnp.float32)
     square = own * own

time: 16.2 us -> 16.2 us (level)
  no operation moved by 1% of the time
where the time goes in v6:
time: 16.2 us; the launch traced here: 16 us
  Pallas kernels  14.7 us (91%)
  between operations  0.64 us (4%)
  other arithmetic  0.63 us (4%)
    pallas_call x1, Pallas kernels, per_device(): pl.pallas_call(functools.partial(kernel, n, D, H, CH), out_shape=(out, ou...  14.7 us
    add x1, other arithmetic, per_device(): return (norms + lo, norms + se)  0.63 us

profile of v6, /device:TPU:0, one launch (start us, length us, event | category | flops | bytes accessed | tf_op | source)
XLA Modules:
  0.0 16.0 jit_solution(6867067391161697868)
XLA Ops:
  0.6 14.7 %shard_map.30 = (f32[3,1,1024]{2,1,0:T(1,128)S(1)}, f32[3,1,1024]{2,1,0:T(1,128)S(1)}, f32[1,1024]{1,0:T(1,128)S(1)}) custom-call(bf16[512,128]{1,0:T(8,128)(2,1)} %bitcast.3), custom_call_target="tpu_custom_call" | custom-call | tf_op jit(solution)/shard_map/pallas_call | solution.py:559
  15.4 0.6 %broadcast_add_fusion = (f32[3,1,1024]{2,1,0:T(1,128)}, f32[3,1,1024]{2,1,0:T(1,128)}) fusion(f32[3,1,1024]{2,1,0:T(1,128)S(1)} %get-tuple-element.7, f32[1024]{0:T(1024)S(1)} %bitcast.2, f32[3,1,1024]{2,1,0:T(1,128)S(1)} %get-tuple-element.6), kind=kLoop, calls=%fused_computation | loop fusion | flops 6144 | bytes 53248 | tf_op jit(solution)/shard_map/add | solution.py:592
